TPU v7x, 256 devices: a whole 4x4x8 slice. The times are simulated.
256 devices in a mesh: img: 64 (over y, z, core), nrn: 4 (over x).
Axes of the slice: x: 4, y: 4, z: 8, core: 2. Of those that a mesh axis runs over, the one named last changes fastest.
Arguments:
- images: bfloat16 [16384, 16384], P('img', 'nrn'), may hold values from 0 to 12
- weights: bfloat16 [2, 128, 512, 128], P(None, 'nrn'), may hold values from -0.375 to 0.375
- block_index: int32 [2, 128, 4], replicated, may hold values from 0 to 127, as said below
- bias: float32 [2, 16384], replicated, may hold values from -0.2 to -0.02
Outputs:
- activations: bfloat16 [16384, 16384], P('img', 'nrn')
- live_fraction: float32 [2], replicated
Inputs may be any that keep to these rules, and one draw needn't show every extreme that they name: `block_index`: the 4 entries of each row name different blocks.
All inputs are finite; a program needn't handle non-finite values.
Results may differ from a plain program's by a relative error of at most 0.005.
Values may be sent and summed in bfloat16 or wider, within the bound.
A program may use at most 128 MiB of HBM per device.

v0:
```python
import jax
import jax.numpy as jnp
from jax import lax
from jax.sharding import PartitionSpec as P

live_level = 0.25


def copy_for_each(array, axis):
    copies = jnp.broadcast_to(array, (lax.axis_size(axis), *array.shape))
    return lax.all_to_all(copies, axis, split_axis=0, concat_axis=0, tiled=True)


def taken_together(array, axis):
    return copy_for_each(array, axis).sum(axis=0)


def select_product(full_rows, tiles, chosen, offsets):
    count = full_rows.shape[0]
    width = tiles.shape[-1]
    blocked = full_rows.reshape(count, full_rows.shape[1] // width, width)
    picked = jnp.take(blocked, chosen.reshape(-1), axis=1).reshape(
        count, tiles.shape[0], tiles.shape[1]
    )
    result = jnp.einsum("brk,rkc->brc", picked, tiles, preferred_element_type=jnp.float32)
    result = result.reshape(count, tiles.shape[0] * width) + offsets
    return jnp.maximum(result, 0.0).astype(jnp.bfloat16)


def per_device(images, weights, block_index, bias):
    layers_total = weights.shape[0]
    neuron_shard = images.shape[1]
    rows_here = weights.shape[1]
    neurons_total = neuron_shard * lax.axis_size("nrn")
    tokens_total = images.shape[0] * lax.axis_size("img")
    position = lax.axis_index("nrn")
    current = images
    partial_list = []
    for layer_no in range(layers_total):
        whole = lax.all_gather(current, "nrn", axis=1, tiled=True)
        chosen = lax.dynamic_slice_in_dim(block_index[layer_no], position * rows_here, rows_here, 0)
        offsets = lax.dynamic_slice_in_dim(bias[layer_no], position * neuron_shard, neuron_shard, 0)
        current = select_product(whole, weights[layer_no], chosen, offsets)
        partial_value = jnp.sum(current.astype(jnp.float32), axis=1)
        partial_list.append(partial_value)
    totals = taken_together(jnp.stack(partial_list), "nrn")
    shares = jnp.sum(jnp.minimum(1.0, totals / neurons_total / live_level), axis=1)
    live = taken_together(shares, "img")
    return (current, live / tokens_total)


def solution(mesh):
    in_specs = (P("img", "nrn"), P(None, "nrn", None, None), P(), P())
    out_specs = (P("img", "nrn"), P())
    return jax.shard_map(
        per_device, mesh=mesh, in_specs=in_specs, out_specs=out_specs, check_vma=False
    )
```

profile of v0, /device:TPU:1, one launch (start us, length us, event | category | flops | bytes accessed | tf_op | source)
XLA Modules:
  0.0 324.9 jit_solution(8266129144702667340)
XLA Ops:
  7.2 0.0 copy-start.1
  7.2 0.0 copy-start
  7.2 0.0 all-gather.3.cloned.1.call-start
  7.2 4.1 %copy.48 = bf16[256,4096]{0,1:T(8,128)(2,1)} copy(bf16[256,4096]{1,0:T(8,128)(2,1)} %param.6) | data formatting | bytes 4194304 | tf_op args[0]
  11.3 0.0 all-gather.3.cloned.1.call-update
  11.4 0.0 all-gather.5.cloned.1.call-start
  11.4 0.0 copy-done.1
  11.4 0.1 constant_dynamic-slice_fusion.3
  11.5 0.1 copy.47
  11.6 0.1 reshape.56
  11.7 0.1 constant_dynamic-slice_fusion.1
  11.8 0.1 copy.46
  11.9 0.1 reshape.60
  12.0 0.0 copy-done
  12.0 0.1 fusion.14
  12.2 88.6 %all-gather.3.cloned.1.call-done = bf16[256,16384]{0,1:T(8,128)(2,1)} async-done(((bf16[256,4096]{0,1:T(8,128)(2,1)}), bf16[256,16384]{0,1:T(8,128)(2,1)}) %all-gather.3.cloned.1.call-update) | async-done | bytes 8388624 | tf_op jit(solution)/shard_map/all_gather | solution.py:40
  100.7 11.9 %copy.49 = bf16[256,128,128]{2,0,1:T(8,128)(2,1)} copy(bf16[256,128,128]{0,2,1:T(8,128)(2,1)} %bitcast.60) | data formatting | bytes 16777216 | tf_op jit(solution)/shard_map/reshape | solution.py:21
  112.7 10.0 %gather_fusion = bf16[128,256,128]{2,1,0:T(8,128)(2,1)} fusion(bf16[256,128,128]{2,0,1:T(8,128)(2,1)} %copy.49, s32[1024]{0:T(1024)S(1)} %pad_clamp_fusion.1), kind=kCustom, calls=%fused_computation.clone | custom fusion | bytes 16777728 | tf_op jit(solution)/shard_map/jit(_take)/gather | solution.py:22
  122.6 7.4 %select_bitcast_fusion.1 = bf16[256,128,128]{2,0,1:T(8,128)(2,1)} fusion(bf16[128,256,128]{2,1,0:T(8,128)(2,1)} %gather_fusion, pred[128]{0:T(512)(128)(4,1)S(1)} %get-tuple-element.20), kind=kLoop, calls=%fused_computation.3 | loop fusion | flops 4194304 | bytes 16777344 | tf_op jit(solution)/shard_map/jit(_take)/select_n | solution.py:22
  130.0 11.9 %copy.50 = bf16[256,128,128]{0,2,1:T(8,128)(2,1)} copy(bf16[256,128,128]{2,0,1:T(8,128)(2,1)} %select_bitcast_fusion.1) | data formatting | bytes 16777216 | tf_op jit(solution)/shard_map/jit(_take)/select_n | solution.py:22
  142.0 6.9 %convert_reduce_fusion.1 = (f32[256]{0:T(256)S(1)}, f32[32,256,128]{1,2,0:T(8,128)S(1)}) fusion(f32[32,128]{1,0:T(8,128)S(1)} %bitcast.64, bf16[256,32,512]{0,2,1:T(8,128)(2,1)} %bitcast.59, bf16[2,32,512,128]{3,2,1,0:T(8,128)(2,1)} %param.7), kind=kOutput, calls=%fused_computation.21 | convolution fusion | flops 1078984448 | bytes 16794624 | tf_op jit(solution)/shard_map/brk,rkc->brc/dot_general | solution.py:25
  148.8 2.0 fusion.7
  150.8 0.0 all-gather.5.cloned.1.call-update
  150.9 86.7 %all-gather.5.cloned.1.call-done = bf16[256,16384]{0,1:T(8,128)(2,1)} async-done(((bf16[256,4096]{0,1:T(8,128)(2,1)}), bf16[256,16384]{0,1:T(8,128)(2,1)}) %all-gather.5.cloned.1.call-update) | async-done | bytes 8388624 | tf_op jit(solution)/shard_map/all_gather | solution.py:40
  237.6 11.9 %copy.53 = bf16[256,128,128]{2,0,1:T(8,128)(2,1)} copy(bf16[256,128,128]{0,2,1:T(8,128)(2,1)} %bitcast.61) | data formatting | bytes 16777216 | tf_op jit(solution)/shard_map/reshape | solution.py:21
  249.5 10.0 %gather_fusion.1 = bf16[128,256,128]{2,1,0:T(8,128)(2,1)} fusion(bf16[256,128,128]{2,0,1:T(8,128)(2,1)} %copy.53, s32[1024]{0:T(1024)S(1)} %pad_clamp_fusion), kind=kCustom, calls=%fused_computation.1.clone | custom fusion | bytes 16777728 | tf_op jit(solution)/shard_map/jit(_take)/gather | solution.py:22
  259.5 7.4 %select_bitcast_fusion = bf16[256,128,128]{2,0,1:T(8,128)(2,1)} fusion(bf16[128,256,128]{2,1,0:T(8,128)(2,1)} %gather_fusion.1, pred[128]{0:T(512)(128)(4,1)S(1)} %get-tuple-element.19), kind=kLoop, calls=%fused_computation.2 | loop fusion | flops 4194304 | bytes 16777344 | tf_op jit(solution)/shard_map/jit(_take)/select_n | solution.py:22
  266.9 11.9 %copy.54 = bf16[256,128,128]{0,2,1:T(8,128)(2,1)} copy(bf16[256,128,128]{2,0,1:T(8,128)(2,1)} %select_bitcast_fusion) | data formatting | bytes 16777216 | tf_op jit(solution)/shard_map/jit(_take)/select_n | solution.py:22
  278.8 8.7 %convert_reduce_fusion = (f32[256]{0:T(256)S(1)}, f32[32,256,128]{1,2,0:T(8,128)}) fusion(f32[32,128]{1,0:T(8,128)S(1)} %bitcast.62, bf16[256,32,512]{0,2,1:T(8,128)(2,1)} %bitcast.58, bf16[2,32,512,128]{3,2,1,0:T(8,128)(2,1)} %param.7), kind=kOutput, calls=%fused_computation.20 | convolution fusion | flops 1078984448 | bytes 16794624 | tf_op jit(solution)/shard_map/brk,rkc->brc/dot_general | solution.py:25
  287.5 7.6 %all_to_all.11 = f32[4,2,256]{2,1,0:T(2,128)S(1)} all-to-all(f32[4,2,256]{2,1,0:T(2,128)S(1)} %broadcast_in_dim.17), channel_id=1, replica_groups=mesh['img'=64,'nrn'=4] {'nrn'}, dimensions={0} | all-to-all | bytes 16384 | tf_op jit(solution)/shard_map/all_to_all | solution.py:11
  295.2 0.1 minimum_reduce_fusion
  295.3 0.6 broadcast_in_dim.18
  295.9 12.3 %all-to-all-start.1 = ((f32[64,1,2]{2,1,0:T(1,128)}), f32[64,1,2]{2,1,0:T(1,128)S(1)}, u32[]{:S(2)}, u32[]{:S(2)}) async-start(f32[64,1,2]{2,1,0:T(1,128)} %broadcast_in_dim.18), calls=%async_computation.1 | async-start | bytes 65536 | tf_op jit(solution)/shard_map/all_to_all | solution.py:11
  308.2 2.6 fusion.5
  310.8 2.9 copy.59
  313.7 3.8 %all-to-all-done.1 = f32[64,1,2]{2,1,0:T(1,128)S(1)} async-done(((f32[64,1,2]{2,1,0:T(1,128)}), f32[64,1,2]{2,1,0:T(1,128)S(1)}, u32[]{:S(2)}, u32[]{:S(2)}) %all-to-all-start.1) | async-done | bytes 544 | tf_op jit(solution)/shard_map/all_to_all | solution.py:11
  317.5 0.1 reduce_sum.49
  317.6 0.5 broadcast_multiply_fusion
  (10 shorter events, 0.1 us)
Async XLA Ops:
  7.2 4.3 %copy-start.1 = (s32[2,128,4]{1,2,0:T(4,128)S(1)}, s32[2,128,4]{1,2,0:T(4,128)}, u32[]{:S(2)}) copy-start(s32[2,128,4]{1,2,0:T(4,128)} %param.8) | copy-start | bytes 12292
  7.2 4.9 %copy-start = (f32[2,16384]{1,0:T(2,128)S(1)}, f32[2,16384]{1,0:T(2,128)}, u32[]{:S(2)}) copy-start(f32[2,16384]{1,0:T(2,128)} %param.9) | copy-start | bytes 393220
  7.2 93.5 %all-gather.3.cloned.1.call-start = ((), (), s32[]{:S(2)}) async-start(), calls=%async_computation.2 | async-start | bytes 10485760 | tf_op jit(solution)/shard_map/all_gather | solution.py:40
  11.4 226.2 %all-gather.5.cloned.1.call-start = ((), (), s32[]{:S(2)}) async-start(), calls=%async_computation.3 | async-start | bytes 10485760 | tf_op jit(solution)/shard_map/all_gather | solution.py:40
  295.9 21.6 %all-to-all-start.1 = ((f32[64,1,2]{2,1,0:T(1,128)}), f32[64,1,2]{2,1,0:T(1,128)S(1)}, u32[]{:S(2)}, u32[]{:S(2)}) async-start(f32[64,1,2]{2,1,0:T(1,128)} %broadcast_in_dim.18), calls=%async_computation.1 | async-start | bytes 65536 | tf_op jit(solution)/shard_map/all_to_all | solution.py:11
Sparse Core Ops, SparseCore 0:
  11.5 89.2 all-gather.2
  151.0 86.5 all-gather.4
where the time goes:
time: 326 us; the launch traced here: 325 us
  waiting for transfers between devices  179 us (55%)
  local copies, waits for them, and re-layouts  75.9 us (23%)
  other arithmetic  20.2 us (6%)
  matrix products  15.5 us (5%)
  between operations  14.2 us (4%)
  starting transfers between devices  12.4 us (4%)
  blocking collectives  7.64 us (2%)
    all_gather x2, waiting for transfers between devices, per_device(): whole = lax.all_gather(current, 'nrn', axis=1, tiled=True)  175 us
    select_n x2, local copies, waits for them, and re-layouts, select_product(): jnp.take(blocked, chosen.reshape(-1), axis=1)  23.9 us
    reshape x2, local copies, waits for them, and re-layouts, select_product(): blocked = full_rows.reshape(count, full_rows.shape[1] // width, width)  23.9 us
    gather x2, local copies, waits for them, and re-layouts, select_product(): jnp.take(blocked, chosen.reshape(-1), axis=1)  19.9 us
    dot_general x2, matrix products, select_product(): jnp.einsum('brk,rkc->brc', picked, tiles, preferred_element_type=jnp.floa...  15.5 us
    select_n x4, other arithmetic, select_product(): jnp.take(blocked, chosen.reshape(-1), axis=1)  14.8 us
    all_to_all x1, starting transfers between devices, copy_for_each(): return lax.all_to_all(copies, axis, split_axis=0, concat_axis=0, tiled=True)  12.3 us
    all_to_all x1, blocking collectives, copy_for_each(): return lax.all_to_all(copies, axis, split_axis=0, concat_axis=0, tiled=True)  7.64 us
  transfers between devices with their start and end apart: 3, of which 3 were waited for; matrix products, arithmetic and copies ran while one was open for 2% of the time, Pallas kernels for 0%

commit v1 on v0

v1 whole, which is shorter than its diff:
```python
import jax
import jax.numpy as jnp
from jax import lax
from jax.experimental import pallas as pl
from jax.experimental.pallas import tpu as pltpu
from jax.sharding import PartitionSpec as P

MESH = pl.DeviceIdType.MESH
LIVE_LEVEL = 0.25
NX, NY, NZ, NW = 4, 4, 8, 4
T = 128


def kernel(img, w, bi, bias, out, stat, im, X, Y1, Wb, Wo, Ob, acc, accr, rz, ry, rx,
           x_ss, x_rs, w_ss, w_rs, y_ss, y_rs, o_ss, o_rs, a_ss, a_rs, l_sem, im_sem, z_ss, z_rs):
    x = lax.axis_index("nrn")
    i = lax.axis_index("img")
    c = i % 2
    z = (i // 2) % NZ
    y = i // (2 * NZ)
    zm = z % NW
    rows = img.shape[0] // NX
    cols = img.shape[1]
    per_x = w.shape[1]
    half = per_x // 2
    kk = w.shape[2]
    hk, qk = kk // 2, kk // 4

    def dev(dx=0, dy=0, dz=0, s=0):
        cc = (c + s) % 2
        return (((y + dy + NY) % NY) * 2 * NZ + ((z + dz + NZ) % NZ) * 2 + cc, (x + dx + NX) % NX)

    def rc(src, dst, ss, rs, d):
        return pltpu.make_async_remote_copy(src_ref=src, dst_ref=dst, send_sem=ss, recv_sem=rs,
                                            device_id=d, device_id_type=MESH)

    partners = [dev(s=1), dev(dy=1), dev(dy=-1), dev(dz=1), dev(dz=-1)]
    partners += [dev(dx=d, s=s) for d in (1, 2, 3) for s in (0, 1)]
    partners += [dev(dz=d) for d in range(2, NZ - 1)] + [dev(dy=2)]
    bar = pltpu.get_barrier_semaphore()
    for p in partners:
        pl.semaphore_signal(bar, 1, device_id=p, device_id_type=MESH)
    pl.semaphore_wait(bar, len(partners))

    def xrow(g):
        return pl.ds(pl.multiple_of(g * rows, rows), rows)

    def xblk(q):
        return pl.ds(q * per_x, per_x)

    def xa_send(d):
        t = (x + d) % NX
        return rc(im.at[:, xrow(t), :], X.at[xblk(x), xrow(c), :], x_ss.at[d], x_rs.at[d], dev(dx=d))

    def xa_recv(d):
        q = (x - d + NX) % NX
        return rc(im.at[:, xrow(x), :], X.at[xblk(q), xrow(c), :], x_ss.at[d], x_rs.at[d], dev(dx=d))

    def xf(d, other=0):
        q = (x - d + NX) % NX
        ref = X.at[xblk(q), xrow((c + other) % 2), :]
        if d == 0 and not other:
            src = im.at[:, xrow(x), :]
        else:
            src = ref
        return rc(src, ref, x_ss.at[3 + d + (d == 0) * 4], x_rs.at[3 + d + (d == 0) * 4], dev(s=1))

    j0 = y * NW + zm

    def xi(l, d):
        return rc(w.at[l, c * half + j0], Wb.at[l, d - 1, 0, 0], w_ss.at[l, d - 1], w_rs.at[l, d - 1], dev(dx=-d))

    def part(l, st, ey, ez, lo, n):
        return Wb.at[l, :, ey, ez, pl.ds(lo, n), :]

    def msgs(l, half_b):
        lo = hk if half_b else 0
        so = 3 + (8 if half_b else 0)
        ro = 3 + (20 if half_b else 0)

        def slot(a, b, lo_, n):
            return part(l, None, b, a, lo_, n) if half_b else part(l, None, a, b, lo_, n)

        up1, dn1 = (dev(dz=1), dev(dz=-1)) if half_b else (dev(dy=1), dev(dy=-1))
        up2, dn2 = (dev(dy=1), dev(dy=-1)) if half_b else (dev(dz=1), dev(dz=-1))
        ws, wr = w_ss, w_rs
        m = {}
        m["1p"] = rc(slot(0, 0, lo, hk), slot(3, 0, lo, hk), ws.at[l, so], wr.at[l, ro], up1)
        m["1m"] = rc(slot(0, 0, lo, hk), slot(1, 0, lo, hk), ws.at[l, so + 1], wr.at[l, ro + 1], dn1)
        m["1fp"] = rc(slot(3, 0, lo, qk), slot(2, 0, lo, qk), ws.at[l, so + 2], wr.at[l, ro + 2], up1)
        m["1fm"] = rc(slot(1, 0, lo + qk, qk), slot(2, 0, lo + qk, qk), ws.at[l, so + 3], wr.at[l, ro + 3], dn1)
        for e in range(4):
            m["2p", e] = rc(slot(e, 0, lo, hk), slot(e, 3, lo, hk), ws.at[l, so + 4], wr.at[l, ro + 4 + e], up2)
            m["2m", e] = rc(slot(e, 0, lo, hk), slot(e, 1, lo, hk), ws.at[l, so + 5], wr.at[l, ro + 8 + e], dn2)
            m["2fp", e] = rc(slot(e, 3, lo, qk), slot(e, 2, lo, qk), ws.at[l, so + 6], wr.at[l, ro + 12 + e], up2)
            m["2fm", e] = rc(slot(e, 1, lo + qk, qk), slot(e, 2, lo + qk, qk), ws.at[l, so + 7], wr.at[l, ro + 16 + e], dn2)
        def allsl(b, lo_, n):
            return Wb.at[l, :, b, :, pl.ds(lo_, n), :] if half_b else Wb.at[l, :, :, b, pl.ds(lo_, n), :]
        m["sends"] = [m["1p"], m["1m"], m["1fp"], m["1fm"]]
        for b, o, n, k in ((0, 0, hk, 4), (0, 0, hk, 5), (3, 0, qk, 6), (1, qk, qk, 7)):
            r = allsl(b, lo + o, n)
            m["sends"].append(rc(r, r, ws.at[l, so + k], wr.at[l, ro + 4], up2))
        return m

    MA = [msgs(l, False) for l in range(2)]
    MB = [msgs(l, True) for l in range(2)]

    def s0(l):
        for d in (1, 3, 2):
            xi(l, d).wait_recv()
        for k in ("1p", "1m", ("2p", 0), ("2m", 0)):
            MA[l][k].start()
            MB[l][k].start()

    def s1(l):
        for k, e in (("p", 3), ("m", 1)):
            MA[l]["1" + k].wait_recv()
            MB[l]["1" + k].wait_recv()
            MA[l]["1f" + k].start()
            MB[l]["1f" + k].start()
        for e in (3, 1):
            for k in ("2p", "2m"):
                MA[l][k, e].start()
                MB[l][k, e].start()

    def s2(l):
        for k in ("1fp", "1fm"):
            MA[l][k].wait_recv()
            MB[l][k].wait_recv()
        for k in ("2p", "2m"):
            MA[l][k, 2].start()
            MB[l][k, 2].start()

    def s3(l, e):
        for k in ("p", "m"):
            MA[l]["2" + k, e].wait_recv()
            MB[l]["2" + k, e].wait_recv()
            MA[l]["2f" + k, e].start()
            MB[l]["2f" + k, e].start()

    def s4(l, e):
        for k in ("2fp", "2fm"):
            MA[l][k, e].wait_recv()
            MB[l][k, e].wait_recv()

    def block(l, q, j, wt, store):
        src = X if l == 0 else Y1
        r = q * per_x + c * half + j
        xs = [src[bi[l, r, k]] for k in range(kk // T)]
        pre = jnp.dot(jnp.concatenate(xs, axis=1), wt, preferred_element_type=jnp.float32)
        pre = pre + bias[pl.ds(l, 1), pl.ds(pl.multiple_of(r * T, T), T)]
        act = jnp.maximum(pre, 0.0).astype(jnp.bfloat16)
        store(r, act)
        return act.astype(jnp.float32)

    def put(l, d, j):
        def store(r, act):
            if l == 0:
                Y1[r] = act
            else:
                Ob[d, :, pl.ds(pl.multiple_of(j * T, T), T)] = act
        return store

    def own_blocks(l):
        def body(t, _):
            s = acc[l]
            for u in range(2):
                j = t * 2 + u
                s = s + block(l, x, j, Wo[l, j], put(l, 0, j))
            acc[l] = s
            return 0
        lax.fori_loop(0, half // 2, body, 0)

    def slots(l, n, fey, fez):
        def body(t, _):
            ey, ez = fey(t), fez(t)
            j = ((y + ey) % NY) * NW + (zm + ez) % NW
            s = acc[l]
            for d in (1, 2, 3):
                s = s + block(l, (x + d) % NX, j, Wb[l, d - 1, ey, ez], put(l, d, j))
            acc[l] = s
            return 0
        lax.fori_loop(0, n, body, 0)

    def osl(q):
        return pl.ds(pl.multiple_of(q * half * T, half * T), half * T)

    def y1x(d, other):
        cc = (c + other) % 2
        q = (x + d) % NX
        ref = Y1.at[pl.ds((q * 2 + cc) * half, half)]
        return rc(ref, ref, y_ss.at[d], y_rs.at[d], dev(s=1))

    def out_send(d, s, j, n=1):
        src = Ob.at[d, xrow((c + s) % 2), pl.ds(pl.multiple_of(j * T, T), n * T)]
        dst = out.at[xrow(x), pl.ds(pl.multiple_of((c * half + j) * T, T), n * T)]
        if d == 0 and s == 0:
            return pltpu.make_async_copy(src, dst, l_sem.at[3])
        return rc(src, dst, o_ss.at[d, s], o_rs.at[d, s], dev(dx=d, s=s))

    def out_wait(d, s, recv):
        if recv:
            ref = out.at[xrow((x - d + NX) % NX), osl((c + s) % 2)]
            rc(ref, ref, o_ss.at[d, s], o_rs.at[d, s], dev(dx=d, s=s)).wait_recv()
        else:
            ref = Ob.at[d, xrow((c + s) % 2), :]
            rc(ref, ref, o_ss.at[d, s], o_rs.at[d, s], dev(dx=d, s=s)).wait_send()

    def send_slots(pairs):
        for ey, ez in pairs:
            j = ((y + ey) % NY) * NW + (zm + ez) % NW
            for d in (1, 3, 2):
                for s in (0, 1):
                    out_send(d, s, j).start()

    for d in (1, 3, 2):
        xi(0, d).start()
    imc = [pltpu.make_async_copy(img.at[:, pl.ds(b * T, T)], im.at[b], im_sem) for b in range(per_x)]
    for cp in imc:
        cp.start()
    pltpu.make_async_copy(im, im, im_sem).wait()
    for d in (1, 3, 2):
        xa_send(d).start()
    xf(0).start()
    for d in (1, 3, 2):
        xi(1, d).start()
    local = [pltpu.make_async_copy(w.at[l, pl.ds(pl.multiple_of(c * half, half), half)], Wo.at[l], l_sem.at[l])
             for l in range(2)]
    local.append(pltpu.make_async_copy(im.at[:, xrow(x), :], X.at[xblk(x), xrow(c), :], l_sem.at[2]))
    for cp in local:
        cp.start()
    acc[...] = jnp.zeros_like(acc)

    s0(0)
    s1(0)
    s3(0, 0)
    s2(0)
    s3(0, 3)
    s3(0, 1)
    for d in (1, 3, 2):
        xa_recv(d).wait_recv()
        xf(d).start()
    s3(0, 2)
    for cp in local:
        cp.wait()
    for d in (0, 1, 3, 2):
        xf(d, other=1).wait_recv()
    s0(1)
    own_blocks(0)
    for e in range(4):
        s4(0, e)
    y1x(0, 0).start()
    slots(0, 4, lambda t: 0, lambda t: t)
    s1(1)
    slots(0, 4, lambda t: 1, lambda t: t)
    s3(1, 0)
    slots(0, 8, lambda t: 2 + t // 4, lambda t: t % 4)
    s2(1)
    for d in (1, 2, 3):
        y1x(d, 0).start()
    s3(1, 3)
    for d in range(4):
        y1x(d, 1).wait_recv()
    own_blocks(1)
    slots(1, 1, lambda t: 0, lambda t: 0)
    s3(1, 1)
    for s in (0, 1):
        out_send(0, s, 0, half).start()
    send_slots([(0, 0)])
    slots(1, 2, lambda t: 0, lambda t: 1 + 2 * t)
    slots(1, 2, lambda t: 1 + 2 * t, lambda t: 0)
    send_slots([(0, 1), (0, 3), (1, 0), (3, 0)])
    s3(1, 2)
    slots(1, 4, lambda t: 1 + 2 * (t // 2), lambda t: 1 + 2 * (t % 2))
    s4(1, 0)
    send_slots([(1, 1), (1, 3), (3, 1), (3, 3)])
    slots(1, 2, lambda t: 2 * t, lambda t: 2 - 2 * t)
    s4(1, 3)
    s4(1, 1)
    send_slots([(0, 2), (2, 0)])
    slots(1, 2, lambda t: 1 + 2 * t, lambda t: 2)
    slots(1, 2, lambda t: 2, lambda t: 1 + 2 * t)
    send_slots([(1, 2), (3, 2), (2, 1), (2, 3)])
    s4(1, 2)
    slots(1, 1, lambda t: 2, lambda t: 2)

    ax = rc(acc.at[:, xrow((c + 1) % 2), :], accr, a_ss.at[0], a_rs.at[0], dev(s=1))
    send_slots([(2, 2)])
    ax.start()
    mine = acc[:, xrow(c), :]
    ax.wait_recv()
    tot = jnp.sum(mine + accr[...], axis=2)
    share = jnp.minimum(1.0, tot * (1.0 / (NX * cols * LIVE_LEVEL)))
    part_sum = jnp.broadcast_to(jnp.sum(share, axis=1, keepdims=True), (2, T))

    def gather_sum(buf, n, me, val, targets, base):
        buf[me] = val
        cps = [rc(buf.at[me], buf.at[me], z_ss.at[base + k], z_rs.at[base + k], t) for k, (t, _) in enumerate(targets)]
        for cp in cps:
            cp.start()
        for k, (_, who) in enumerate(targets):
            rc(buf.at[who], buf.at[who], z_ss.at[base + k], z_rs.at[base + k], dev(s=1)).wait_recv()
        total = buf[0]
        for k in range(1, n):
            total = total + buf[k]
        for cp in cps:
            cp.wait_send()
        return total

    v = gather_sum(rz, NZ, z, part_sum, [(dev(dz=d), (z - d + NZ) % NZ) for d in range(1, NZ)], 0)
    v = gather_sum(ry, NY, y, v, [(dev(dy=d), (y - d + NY) % NY) for d in range(1, NY)], NZ)
    me_x = [(dev(dx=d, s=s), ((x - d + NX) % NX) * 2 + (c + s) % 2) for d in range(NX) for s in (0, 1) if d or s]
    v = gather_sum(rx, 2 * NX, x * 2 + c, v, me_x, NZ + NY)
    stat[...] = v * (1.0 / (NX * rows * 2 * NZ * NY))

    for l in range(2):
        for d in (1, 2, 3):
            xi(l, d).wait_send()
        for cp in MA[l]["sends"] + MB[l]["sends"]:
            cp.wait_send()
    for d in (1, 2, 3):
        xa_send(d).wait_send()
    for d in range(4):
        xf(d).wait_send()
        y1x(d, 0).wait_send()
    ax.wait_send()
    out_send(0, 0, 0, half).wait()
    for d in range(4):
        for s in (0, 1):
            if d or s:
                out_wait(d, s, True)
                out_wait(d, s, False)


def per_device(images, weights, block_index, bias):
    n_img, cols = images.shape
    layers, per_x, kk, _ = weights.shape
    rows = n_img // NX
    half = per_x // 2
    total = cols * NX
    dma = pltpu.SemaphoreType.DMA
    any_ = pl.BlockSpec(memory_space=pl.ANY)
    vm = pl.BlockSpec(memory_space=pltpu.VMEM)
    out, stat = pl.pallas_call(
        kernel,
        out_shape=(jax.ShapeDtypeStruct((n_img, cols), jnp.bfloat16), jax.ShapeDtypeStruct((layers, T), jnp.float32)),
        in_specs=[any_, any_, pl.BlockSpec(memory_space=pltpu.SMEM), vm],
        out_specs=(any_, vm),
        scratch_shapes=[
            pltpu.VMEM((per_x, n_img, T), jnp.bfloat16),
            pltpu.VMEM((total // T, 2 * rows, T), jnp.bfloat16),
            pltpu.VMEM((total // T, 2 * rows, T), jnp.bfloat16),
            pltpu.VMEM((layers, 3, NY, NW, kk, T), jnp.bfloat16),
            pltpu.VMEM((layers, half, kk, T), jnp.bfloat16),
            pltpu.VMEM((NX, 2 * rows, half * T), jnp.bfloat16),
            pltpu.VMEM((layers, 2 * rows, T), jnp.float32),
            pltpu.VMEM((layers, rows, T), jnp.float32),
            pltpu.VMEM((NZ, layers, T), jnp.float32),
            pltpu.VMEM((NY, layers, T), jnp.float32),
            pltpu.VMEM((2 * NX, layers, T), jnp.float32),
            dma((8,)), dma((8,)),
            dma((layers, 19)), dma((layers, 43)),
            dma((4,)), dma((4,)),
            dma((4, 2)), dma((4, 2)),
            dma((1,)), dma((1,)),
            dma((4,)), dma,
            dma((20,)), dma((20,)),
        ],
        compiler_params=pltpu.CompilerParams(collective_id=0, has_side_effects=True, vmem_limit_bytes=60 * 1024 * 1024),
        name="sparse_net",
    )(images, weights, block_index, bias)
    return out, stat[:, 0]


def solution(mesh):
    return jax.shard_map(
        per_device, mesh=mesh,
        in_specs=(P("img", "nrn"), P(None, "nrn", None, None), P(), P()),
        out_specs=(P("img", "nrn"), P()), check_vma=False,
    )
```

time: 326 us -> 108 us (0.33)
  waiting for transfers between devices: 179 us -> 0 us
  Pallas kernels: 0 us -> 101 us
  local copies, waits for them, and re-layouts: 75.9 us -> 5.92 us
  other arithmetic: 20.2 us -> 0 us
  matrix products: 15.5 us -> 0 us
  between operations: 14.2 us -> 0.64 us
  starting transfers between devices: 12.4 us -> 0 us
  blocking collectives: 7.64 us -> 0 us
    all_gather x2 -> x0, waiting for transfers between devices: 175 us -> none  [per_device(): whole = lax.all_gather(current, 'nrn', axis=1, tiled=True)]
    pallas_call x0 -> x1, Pallas kernels: none -> 101 us  [per_device(): pl.pallas_call(kernel, out_shape=(jax.ShapeDtypeStruct((n_img, cols), jnp...]
    reshape x4 -> x0, local copies, waits for them, and re-layouts: 24.1 us -> none  [the longest x2 23.9 us: select_product(): blocked = full_rows.reshape(count, full_rows.shape[1] // width, width)]
    select_n x2 -> x0, local copies, waits for them, and re-layouts: 23.9 us -> none  [select_product(): jnp.take(blocked, chosen.reshape(-1), axis=1)]
    gather x2 -> x0, local copies, waits for them, and re-layouts: 19.9 us -> none  [select_product(): jnp.take(blocked, chosen.reshape(-1), axis=1)]
    dot_general x2 -> x0, matrix products: 15.5 us -> none  [select_product(): jnp.einsum('brk,rkc->brc', picked, tiles, preferred_element_type=jnp.floa...]
    select_n x4 -> x0, other arithmetic: 14.8 us -> none  [select_product(): jnp.take(blocked, chosen.reshape(-1), axis=1)]
    all_to_all x1 -> x0, starting transfers between devices: 12.3 us -> none  [copy_for_each(): return lax.all_to_all(copies, axis, split_axis=0, concat_axis=0, tiled=True)]
  transfers between devices with their start and end apart: 3 -> 0, of which waited for: 3 -> 0; matrix products, arithmetic and copies ran while one was open for 2% -> 0% of each run, Pallas kernels for 0% -> 0%
where the time goes in v1:
time: 108 us; the launch traced here: 107 us
  Pallas kernels  101 us (94%)
  local copies, waits for them, and re-layouts  5.92 us (5%)
    pallas_call x1, Pallas kernels, per_device(): pl.pallas_call(kernel, out_shape=(jax.ShapeDtypeStruct((n_img, cols), jnp...  101 us
    unnamed x2, local copies, waits for them, and re-layouts  4.61 us

profile of v1, /device:TPU:1, one launch (start us, length us, event | category | flops | bytes accessed | tf_op | source)
XLA Modules:
  0.0 107.5 jit_solution(6638548104516765798)
XLA Ops:
  0.6 1.5 %copy.7.bi = s32[2,128,4]{2,1,0:T(8,128)} copy(s32[2,128,4]{1,2,0:T(4,128)} %param.6) | data formatting | bytes 8192 | tf_op args[2]
  2.1 100.9 %sparse_net.1 = (bf16[256,4096]{1,0:T(8,128)(2,1)}, f32[2,128]{1,0:T(2,128)}) custom-call(bf16[256,4096]{1,0:T(8,128)(2,1)} %img.1, bf16[2,32,512,128]{3,2,1,0:T(8,128)(2,1)} %w.1, s32[2,128,4]{2,1,0:T(8,128)} %copy.7.bi, f32[2,16384]{1,0:T(2,128)} %bias.1), custom_call_target="tpu_custom_call" | custom-call | tf_op jit(solution)/shard_map/sparse_net/pallas_call | solution.py:344
  103.0 1.3 %slice_reduce_fusion = f32[2]{0:T(128)} fusion(f32[2,128]{1,0:T(2,128)} %get-tuple-element.5), kind=kLoop, calls=%fused_computation | loop fusion | bytes 16 | tf_op jit(solution)/shard_map/slice | solution.py:372
  104.3 3.1 %copy.9 = bf16[256,4096]{1,0:T(8,128)(2,1)} copy(bf16[256,4096]{1,0:T(8,128)(2,1)} %get-tuple-element.8) | data formatting | bytes 4194304

commit v2 on v1

v2 whole, which is shorter than its diff:
```python
import jax
import jax.numpy as jnp
from jax import lax
from jax.experimental import pallas as pl
from jax.experimental.pallas import tpu as pltpu
from jax.sharding import PartitionSpec as P

MESH = pl.DeviceIdType.MESH
LIVE_LEVEL = 0.25
NX, NY, NZ, NW = 4, 4, 8, 4
T = 128


RINGS = {"a0": 0, "b0": 1, "b1": 2, "a1": 3}


def kernel(img, w, bi_hbm, bias_hbm, out, stat, im, X, Y1, Wb, Wo, Ob, acc, accr, rz, ry, rx, bi, bias,
           x_ss, x_rs, xi_ss, xi_rs, far_ss, far_rs, w_ss, w_rs, y_ss, y_rs, o_ss, o_rs, a_ss, a_rs, l_sem, im_sem, z_ss, z_rs):
    x = lax.axis_index("nrn")
    i = lax.axis_index("img")
    c = i % 2
    z = (i // 2) % NZ
    y = i // (2 * NZ)
    zm = z % NW
    rows = img.shape[0] // NX
    cols = img.shape[1]
    per_x = w.shape[1]
    half = per_x // 2
    kk = w.shape[2]

    def dev(dx=0, dy=0, dz=0, s=0):
        cc = (c + s) % 2
        return (((y + dy + NY) % NY) * 2 * NZ + ((z + dz + NZ) % NZ) * 2 + cc, (x + dx + NX) % NX)

    def rc(src, dst, ss, rs, d):
        return pltpu.make_async_remote_copy(src_ref=src, dst_ref=dst, send_sem=ss, recv_sem=rs,
                                            device_id=d, device_id_type=MESH)

    partners = [dev(dx=d, s=s) for d in (2, 1, 3) for s in (0, 1)]
    partners += [dev(dz=1), dev(dz=-1), dev(dy=1), dev(dy=-1), dev(s=1)]
    bar = pltpu.get_barrier_semaphore()
    for p in partners:
        pl.semaphore_signal(bar, 1, device_id=p, device_id_type=MESH)
    imc = [pltpu.make_async_copy(img.at[:, pl.ds(b * T, T)], im.at[b], im_sem) for b in range(per_x)]
    local = [pltpu.make_async_copy(bi_hbm, bi, l_sem.at[2]), pltpu.make_async_copy(bias_hbm, bias, l_sem.at[4])]
    local += [pltpu.make_async_copy(w.at[l, pl.ds(pl.multiple_of(c * half, half), half)], Wo.at[l], l_sem.at[l])
              for l in range(2)]
    for cp in imc + local:
        cp.start()
    pl.semaphore_wait(bar, len(partners))

    def xrow(g):
        return pl.ds(pl.multiple_of(g * rows, rows), rows)

    def xblk(q):
        return pl.ds(q * per_x, per_x)

    def xa_send(d):
        t = (x + d) % NX
        return rc(im.at[:, xrow(t), :], X.at[xblk(x), xrow(c), :], x_ss.at[d], x_rs.at[d], dev(dx=d))

    def xa_recv(d):
        q = (x - d + NX) % NX
        return rc(im.at[:, xrow(x), :], X.at[xblk(q), xrow(c), :], x_ss.at[d], x_rs.at[d], dev(dx=d))

    def xf(d, other=0):
        q = (x - d + NX) % NX
        ref = X.at[xblk(q), xrow((c + other) % 2), :]
        src = im.at[:, xrow(x), :] if d == 0 and not other else ref
        k = 4 + d
        return rc(src, ref, x_ss.at[k], x_rs.at[k], dev(s=1))

    j0 = y * NW + zm

    def place(ey, ez):
        return ((y + ey) % NY) * NW + (zm + ez) % NW

    def xi(l, d):
        return rc(Wo.at[l, j0], Wb.at[l, d - 1, 0, 0], xi_ss.at[l, d - 1], xi_rs.at[l, d - 1], dev(dx=-d))

    FAR = ((2, 0), (2, 2), (0, 2), (1, 2), (3, 2))

    def far(h, k):
        a, b = FAR[k]
        d = (1, 3)[h]
        ey, ez = (b, a) if h else (a, b)
        return rc(Wo.at[1, place(ey, ez)], Wb.at[1, d - 1, ey, ez], far_ss.at[h, k], far_rs.at[h, k], dev(dx=-d))

    def ring(name):
        n, l = RINGS[name], int(name[1])
        halves = []
        for h in (0, 1):
            if name[0] == "a":
                d, lo, size = (1, 3)[h], 0, kk
            else:
                d, lo, size = 2, h * (kk // 2), kk // 2
            q = size // 2

            def slot(a, b, off, m, d=d, h=h, lo=lo):
                ey, ez = (b, a) if h else (a, b)
                return Wb.at[l, d - 1, ey, ez, pl.ds(lo + off, m), :]

            up1, dn1, up2, dn2 = dev(dy=1), dev(dy=-1), dev(dz=1), dev(dz=-1)
            if h:
                up1, dn1, up2, dn2 = up2, dn2, up1, dn1
            ss, rs = w_ss.at[n, h], w_rs.at[n, h]
            m = {}
            m["1p"] = rc(slot(0, 0, 0, size), slot(3, 0, 0, size), ss.at[0], rs.at[0], up1)
            m["1m"] = rc(slot(0, 0, 0, size), slot(1, 0, 0, size), ss.at[1], rs.at[1], dn1)
            m["1fp"] = rc(slot(3, 0, 0, q), slot(2, 0, 0, q), ss.at[2], rs.at[2], up1)
            m["1fm"] = rc(slot(1, 0, q, q), slot(2, 0, q, q), ss.at[3], rs.at[3], dn1)
            for e in range(4):
                m["2p", e] = rc(slot(e, 0, 0, size), slot(e, 3, 0, size), ss.at[4], rs.at[4 + e], up2)
                m["2m", e] = rc(slot(e, 0, 0, size), slot(e, 1, 0, size), ss.at[5], rs.at[8 + e], dn2)
                m["2fp", e] = rc(slot(e, 3, 0, q), slot(e, 2, 0, q), ss.at[6], rs.at[12 + e], up2)
                m["2fm", e] = rc(slot(e, 1, q, q), slot(e, 2, q, q), ss.at[7], rs.at[16 + e], dn2)
            sends = [m["1p"], m["1m"], m["1fp"], m["1fm"]]
            for k, b, off, size_k in ((4, 0, 0, size), (5, 0, 0, size), (6, 3, 0, q), (7, 1, q, q)):
                r = slot(slice(None), b, off, size_k)
                sends.append(rc(r, r, ss.at[k], rs.at[4], up2))
            m["sends"] = sends[:2] + sends[4:6] if name == "a1" else sends
            halves.append(m)
        return halves

    R = {name: ring(name) for name in RINGS}

    def t0(name):
        for d in (1, 3) if name[0] == "a" else (2,):
            xi(int(name[1]), d).wait_recv()
        for k in ("1p", "1m", ("2p", 0), ("2m", 0)):
            for m in R[name]:
                m[k].start()

    def t1(name):
        for k in "pm":
            for m in R[name]:
                m["1" + k].wait_recv()
            for m in R[name]:
                m["1f" + k].start()
        for e in (3, 1):
            for k in ("2p", "2m"):
                for m in R[name]:
                    m[k, e].start()

    def t2(name):
        for k in ("1fp", "1fm"):
            for m in R[name]:
                m[k].wait_recv()
        for k in ("2p", "2m"):
            for m in R[name]:
                m[k, 2].start()

    def t3(name, e):
        for k in "pm":
            for m in R[name]:
                m["2" + k, e].wait_recv()
            for m in R[name]:
                m["2f" + k, e].start()

    def t4(name, e):
        for k in ("2fp", "2fm"):
            for m in R[name]:
                m[k, e].wait_recv()

    def block(l, d, j, wt):
        src = X if l == 0 else Y1
        r = ((x + d) % NX) * per_x + c * half + j
        xs = [src[bi[l * (kk // T) + k, r]] for k in range(kk // T)]
        pre = jnp.dot(jnp.concatenate(xs, axis=1), wt, preferred_element_type=jnp.float32)
        pre = pre + bias[pl.ds(l, 1), pl.ds(pl.multiple_of(r * T, T), T)]
        act = jnp.maximum(pre, 0.0).astype(jnp.bfloat16)
        if l == 0:
            Y1[r] = act
        else:
            Ob[d, :, pl.ds(pl.multiple_of(j * T, T), T)] = act
        return act.astype(jnp.float32)

    def loop(l, n, step):
        def body(t, _):
            acc[l] = step(t, acc[l])
            return 0
        lax.fori_loop(0, n, body, 0)

    def own(l, lo=0, n=half):
        def step(t, s):
            for u in range(2):
                j = lo + t * 2 + u
                s = s + block(l, 0, j, Wo[l, j])
            return s
        loop(l, n // 2, step)

    def comp_a(l, n, fa, fb):
        def step(t, s):
            a, b = fa(t), fb(t)
            s = s + block(l, 1, place(a, b), Wb[l, 0, a, b])
            return s + block(l, 3, place(b, a), Wb[l, 2, b, a])
        loop(l, n, step)

    def comp_b(l, n, fa, fb):
        def step(t, s):
            a, b = fa(t), fb(t)
            s = s + block(l, 2, place(a, b), Wb[l, 1, a, b])
            return s + block(l, 2, place(b, a), Wb[l, 1, b, a])
        loop(l, n, step)

    def comp_b_rows(l, ey):
        def step(t, s):
            for u in range(2):
                s = s + block(l, 2, place(ey, t * 2 + u), Wb[l, 1, ey, t * 2 + u])
            return s
        loop(l, 2, step)

    def diag_b(l):
        def step(t, s):
            for u in range(2):
                e = t * 2 + u
                s = s + block(l, 2, place(e, e), Wb[l, 1, e, e])
            return s
        loop(l, 2, step)

    def osl(q):
        return pl.ds(pl.multiple_of(q * half * T, half * T), half * T)

    def y1x(d, other):
        ref = Y1.at[pl.ds((((x + d) % NX) * 2 + (c + other) % 2) * half, half)]
        return rc(ref, ref, y_ss.at[d], y_rs.at[d], dev(s=1))

    def out_send(d, s, j, n=1):
        src = Ob.at[d, xrow((c + s) % 2), pl.ds(pl.multiple_of(j * T, T), n * T)]
        dst = out.at[xrow(x), pl.ds(pl.multiple_of((c * half + j) * T, T), n * T)]
        if d == 0 and s == 0:
            return pltpu.make_async_copy(src, dst, l_sem.at[3])
        return rc(src, dst, o_ss.at[d, s], o_rs.at[d, s], dev(dx=d, s=s))

    def out_wait(d, s, recv):
        if recv:
            ref = out.at[xrow((x - d + NX) % NX), osl((c + s) % 2)]
            rc(ref, ref, o_ss.at[d, s], o_rs.at[d, s], dev(dx=d, s=s)).wait_recv()
        else:
            ref = Ob.at[d, xrow((c + s) % 2), :]
            rc(ref, ref, o_ss.at[d, s], o_rs.at[d, s], dev(dx=d, s=s)).wait_send()

    def send_a(pairs):
        for a, b in pairs:
            for s in (0, 1):
                out_send(1, s, place(a, b)).start()
                out_send(3, s, place(b, a)).start()

    def send_b(pairs):
        for a, b in pairs:
            for s in (0, 1):
                out_send(2, s, place(a, b)).start()

    def start_xi(l, ds):
        for d in ds:
            xi(l, d).start()

    acc[...] = jnp.zeros_like(acc)
    local[2].wait()
    start_xi(0, (1, 3))
    pltpu.make_async_copy(im, im, im_sem).wait()
    xa_send(1).start()
    xa_send(3).start()
    start_xi(0, (2,))
    xa_send(2).start()
    xf(0).start()
    mine_x = pltpu.make_async_copy(im.at[:, xrow(x), :], X.at[xblk(x), xrow(c), :], l_sem.at[5])
    mine_x.start()
    for cp in (local[0], local[1], local[3], mine_x):
        cp.wait()
    start_xi(1, (2, 1, 3))
    for k in range(len(FAR)):
        for h in (0, 1):
            far(h, k).start()

    t0("a0")
    t1("a0")
    t3("a0", 0)
    t0("b0")
    t2("a0")
    t3("a0", 3)
    t3("a0", 1)
    t1("b0")
    t3("a0", 2)
    t3("b0", 0)
    t2("b0")
    for d in (1, 3, 2):
        xa_recv(d).wait_recv()
        xf(d).start()
    t3("b0", 3)
    for d in (0, 1, 3, 2):
        xf(d, other=1).wait_recv()
    own(0)
    y1x(0, 0).start()
    t0("b1")
    t3("b0", 1)
    for e in range(4):
        t4("a0", e)
    comp_a(0, 4, lambda t: 0, lambda t: t)
    t3("b0", 2)
    comp_a(0, 4, lambda t: 1, lambda t: t)
    t1("b1")
    comp_a(0, 8, lambda t: 2 + t // 4, lambda t: t % 4)
    y1x(1, 0).start()
    y1x(3, 0).start()
    for e in range(4):
        t4("b0", e)
    for ey in range(4):
        comp_b_rows(0, ey)
    y1x(2, 0).start()
    t3("b1", 0)
    t2("b1")
    t0("a1")
    t3("b1", 3)
    t3("b1", 1)
    for h in (0, 1):
        far(h, 0).wait_recv()
        for k in ("2p", "2m"):
            R["a1"][h][k, 2].start()
    for d in range(4):
        y1x(d, 1).wait_recv()
    comp_b(1, 1, lambda t: 0, lambda t: 1)
    comp_b(1, 1, lambda t: 0, lambda t: 3)
    send_b([(0, 1), (1, 0), (0, 3), (3, 0)])
    t3("b1", 2)
    comp_b(1, 1, lambda t: 1, lambda t: 3)
    send_b([(1, 3), (3, 1)])
    for k in range(1, len(FAR)):
        for h in (0, 1):
            far(h, k).wait_recv()
    comp_a(1, 2, lambda t: 2 * t, lambda t: 0)
    send_a([(0, 0), (2, 0)])
    comp_a(1, 4, lambda t: t, lambda t: 2)
    send_a([(0, 2), (1, 2), (2, 2), (3, 2)])
    for k in "pm":
        for m in R["a1"]:
            m["1" + k].wait_recv()
    for e in (3, 1):
        for k in ("2p", "2m"):
            for m in R["a1"]:
                m[k, e].start()
    for e in (0, 3, 1, 2):
        t4("b1", e)
    comp_b(1, 1, lambda t: 0, lambda t: 2)
    comp_b(1, 2, lambda t: 1 + 2 * t, lambda t: 2)
    diag_b(1)
    send_b([(0, 2), (2, 0), (0, 0), (1, 1), (2, 2), (3, 3), (1, 2), (2, 1), (3, 2), (2, 3)])
    comp_a(1, 2, lambda t: 1 + 2 * t, lambda t: 0)
    send_a([(1, 0), (3, 0)])
    own(1)
    for s in (0, 1):
        out_send(0, s, 0, half).start()
    for e, ce in ((0, lambda t: 0), (2, lambda t: 2), (3, lambda t: 3), (1, lambda t: 1)):
        for k in "pm":
            for m in R["a1"]:
                m["2" + k, e].wait_recv()
        comp_a(1, 2, ce, lambda t: 1 + 2 * t)
        send_a([(e, 1), (e, 3)])

    ax = rc(acc.at[:, xrow((c + 1) % 2), :], accr, a_ss.at[0], a_rs.at[0], dev(s=1))
    ax.start()
    mine = acc[:, xrow(c), :]
    ax.wait_recv()
    tot = jnp.sum(mine + accr[...], axis=2)
    share = jnp.minimum(1.0, tot * (1.0 / (NX * cols * LIVE_LEVEL)))
    part_sum = jnp.broadcast_to(jnp.sum(share, axis=1, keepdims=True), (2, T))

    def gather_sum(buf, n, me, val, targets, base):
        buf[me] = val
        cps = [rc(buf.at[me], buf.at[me], z_ss.at[base + k], z_rs.at[base + k], t) for k, (t, _) in enumerate(targets)]
        for cp in cps:
            cp.start()
        for k, (_, who) in enumerate(targets):
            rc(buf.at[who], buf.at[who], z_ss.at[base + k], z_rs.at[base + k], dev(s=1)).wait_recv()
        total = buf[0]
        for k in range(1, n):
            total = total + buf[k]
        return total, cps

    far_first = sorted(range(1, NZ), key=lambda d: -min(d, NZ - d))
    v, cz = gather_sum(rz, NZ, z, part_sum, [(dev(dz=d), (z - d + NZ) % NZ) for d in far_first], 0)
    v, cy = gather_sum(ry, NY, y, v, [(dev(dy=d), (y - d + NY) % NY) for d in (2, 1, 3)], NZ)
    me_x = [(dev(dx=d, s=s), ((x - d + NX) % NX) * 2 + (c + s) % 2) for d in (2, 1, 3, 0) for s in (0, 1) if d or s]
    v, cx = gather_sum(rx, 2 * NX, x * 2 + c, v, me_x, NZ + NY)
    v = v * (1.0 / (NX * rows * 2 * NZ * NY))
    for l in range(2):
        stat[l] = jnp.sum(v[l:l + 1, 0:1])

    for cp in cz + cy + cx:
        cp.wait_send()
    for l in range(2):
        for d in (1, 2, 3):
            xi(l, d).wait_send()
    for h in (0, 1):
        for k in range(len(FAR)):
            far(h, k).wait_send()
    for name in RINGS:
        for m in R[name]:
            for cp in m["sends"]:
                cp.wait_send()
    for d in (1, 2, 3):
        xa_send(d).wait_send()
    for d in range(4):
        xf(d).wait_send()
        y1x(d, 0).wait_send()
    ax.wait_send()
    out_send(0, 0, 0, half).wait()
    for d in range(4):
        for s in (0, 1):
            if d or s:
                out_wait(d, s, True)
                out_wait(d, s, False)


def per_device(images, weights, block_index, bias):
    n_img, cols = images.shape
    layers, per_x, kk, _ = weights.shape
    rows = n_img // NX
    half = per_x // 2
    total = cols * NX
    dma = pltpu.SemaphoreType.DMA
    any_ = pl.BlockSpec(memory_space=pl.ANY)
    index = jnp.transpose(block_index, (0, 2, 1)).reshape(layers * (kk // T), total // T)
    return pl.pallas_call(
        kernel,
        out_shape=(jax.ShapeDtypeStruct((n_img, cols), jnp.bfloat16), jax.ShapeDtypeStruct((layers,), jnp.float32)),
        in_specs=[any_] * 4,
        out_specs=(any_, pl.BlockSpec(memory_space=pltpu.SMEM)),
        scratch_shapes=[
            pltpu.VMEM((per_x, n_img, T), jnp.bfloat16),
            pltpu.VMEM((total // T, 2 * rows, T), jnp.bfloat16),
            pltpu.VMEM((total // T, 2 * rows, T), jnp.bfloat16),
            pltpu.VMEM((layers, 3, NY, NW, kk, T), jnp.bfloat16),
            pltpu.VMEM((layers, half, kk, T), jnp.bfloat16),
            pltpu.VMEM((NX, 2 * rows, half * T), jnp.bfloat16),
            pltpu.VMEM((layers, 2 * rows, T), jnp.float32),
            pltpu.VMEM((layers, rows, T), jnp.float32),
            pltpu.VMEM((NZ, layers, T), jnp.float32),
            pltpu.VMEM((NY, layers, T), jnp.float32),
            pltpu.VMEM((2 * NX, layers, T), jnp.float32),
            pltpu.SMEM(index.shape, jnp.int32),
            pltpu.VMEM(bias.shape, jnp.float32),
            dma((8,)), dma((8,)),
            dma((layers, 3)), dma((layers, 3)),
            dma((2, 5)), dma((2, 5)),
            dma((4, 2, 8)), dma((4, 2, 20)),
            dma((4,)), dma((4,)),
            dma((4, 2)), dma((4, 2)),
            dma((1,)), dma((1,)),
            dma((6,)), dma,
            dma((20,)), dma((20,)),
        ],
        compiler_params=pltpu.CompilerParams(collective_id=0, has_side_effects=True, vmem_limit_bytes=60 * 1024 * 1024),
        name="sparse_net",
    )(images, weights, index, bias)


def solution(mesh):
    return jax.shard_map(
        per_device, mesh=mesh,
        in_specs=(P("img", "nrn"), P(None, "nrn", None, None), P(), P()),
        out_specs=(P("img", "nrn"), P()), check_vma=False,
    )
```

time: 108 us -> 97.3 us (0.901)
  Pallas kernels: 101 us -> 92.9 us
  local copies, waits for them, and re-layouts: 5.92 us -> 3.65 us
    pallas_call x1, Pallas kernels: 101 us -> 92.9 us  [per_device(): pl.pallas_call(kernel, out_shape=(jax.ShapeDtypeStruct((n_img, cols), jnp...]
    slice x1 -> x0, local copies, waits for them, and re-layouts: 1.31 us -> none  [per_device(): return (out, stat[:, 0])]
    unnamed x2 -> x4, local copies, waits for them, and re-layouts: 4.61 us -> 3.65 us
where the time goes in v2:
time: 97.3 us; the launch traced here: 97.1 us
  Pallas kernels  92.9 us (95%)
  local copies, waits for them, and re-layouts  3.65 us (4%)
    pallas_call x1, Pallas kernels, per_device(): pl.pallas_call(kernel, out_shape=(jax.ShapeDtypeStruct((n_img, cols), jnp...  92.9 us
    unnamed x4, local copies, waits for them, and re-layouts  3.65 us

profile of v2, /device:TPU:1, one launch (start us, length us, event | category | flops | bytes accessed | tf_op | source)
XLA Modules:
  0.0 97.1 jit_solution(13511388805511565392)
XLA Ops:
  0.6 92.9 %sparse_net.1 = (bf16[256,4096]{1,0:T(8,128)(2,1)}, f32[2]{0:T(128)}) custom-call(bf16[256,4096]{1,0:T(8,128)(2,1)} %img.1, bf16[2,32,512,128]{3,2,1,0:T(8,128)(2,1)} %w.1, s32[8,128]{1,0:T(8,128)} %bitcast.3, f32[2,16384]{1,0:T(2,128)} %bias_hbm.1), custom_call_target="tpu_custom_call" | custom-call | tf_op jit(solution)/shard_map/sparse_net/pallas_call | solution.py:424
  93.5 0.0 copy-start
  93.5 3.1 %copy.8 = bf16[256,4096]{1,0:T(8,128)(2,1)} copy(bf16[256,4096]{1,0:T(8,128)(2,1)} %get-tuple-element.4) | data formatting | bytes 4194304
  96.6 0.0 copy-done
  96.6 0.5 copy.9
Async XLA Ops:
  93.5 3.1 %copy-start = (f32[2]{0:T(128)S(1)}, f32[2]{0:T(128)}, u32[]{:S(2)}) copy-start(f32[2]{0:T(128)} %get-tuple-element.5) | copy-start | bytes 28

commit v3 on v2

--- a/solution.py
+++ b/solution.py
@@ -11,11 +11,12 @@
 T = 128
 
 
+A1_SENDS = 3
 RINGS = {"a0": 0, "b0": 1, "b1": 2, "a1": 3}
 
 
-def kernel(img, w, bi_hbm, bias_hbm, out, stat, im, X, Y1, Wb, Wo, Ob, acc, accr, rz, ry, rx, bi, bias,
-           x_ss, x_rs, xi_ss, xi_rs, far_ss, far_rs, w_ss, w_rs, y_ss, y_rs, o_ss, o_rs, a_ss, a_rs, l_sem, im_sem, z_ss, z_rs):
+def kernel(img, w, bi_hbm, bias_hbm, out, stat, im, X, Y1, Wb, Wo, Ob, acc, accr, rz, ry, rx, bi, bias, Wx,
+           x_ss, x_rs, xi_ss, xi_rs, xp_rs, x2_ss, x2_rs, far_ss, far_rs, w_ss, w_rs, y_ss, y_rs, o_ss, o_rs, a_ss, a_rs, l_sem, im_sem, wx_sem, z_ss, z_rs):
     x = lax.axis_index("nrn")
     i = lax.axis_index("img")
     c = i % 2
@@ -45,7 +46,8 @@
     local = [pltpu.make_async_copy(bi_hbm, bi, l_sem.at[2]), pltpu.make_async_copy(bias_hbm, bias, l_sem.at[4])]
     local += [pltpu.make_async_copy(w.at[l, pl.ds(pl.multiple_of(c * half, half), half)], Wo.at[l], l_sem.at[l])
               for l in range(2)]
-    for cp in imc + local:
+    first = [pltpu.make_async_copy(w.at[l, c * half + y * NW + zm], Wx.at[l], wx_sem.at[l]) for l in range(2)]
+    for cp in first + imc + local[2:3] + local[:2] + local[3:]:
         cp.start()
     pl.semaphore_wait(bar, len(partners))
 
@@ -76,9 +78,20 @@
         return ((y + ey) % NY) * NW + (zm + ez) % NW
 
     def xi(l, d):
-        return rc(Wo.at[l, j0], Wb.at[l, d - 1, 0, 0], xi_ss.at[l, d - 1], xi_rs.at[l, d - 1], dev(dx=-d))
-
-    FAR = ((2, 0), (2, 2), (0, 2), (1, 2), (3, 2))
+        return rc(Wx.at[l], Wb.at[l, d - 1, 0, 0], xi_ss.at[l, d - 1], xi_rs.at[l, d - 1], dev(dx=-d))
+
+    def xi_part(d, p):
+        r = pl.ds(p * (kk // 2), kk // 2)
+        return rc(Wx.at[0, r, :], Wb.at[0, d - 1, 0, 0, r, :], xi_ss.at[0, d - 1], xp_rs.at[d // 2, p], dev(dx=-d))
+
+    def xi2(l, h):
+        d = (1, 3)[h]
+        r = pl.ds(h * (kk // 2), kk // 2)
+        return rc(Wb.at[l, d - 1, 0, 0, r, :], Wb.at[l, 1, 0, 0, r, :], x2_ss.at[l, h], x2_rs.at[l, h], dev(dx=-d))
+
+    FAR = ((0, 2), (2, 2), (1, 2), (3, 2), (2, 0), (2, 1), (2, 3))
+
+    NF = len(FAR)
 
     def far(h, k):
         a, b = FAR[k]
@@ -116,8 +129,16 @@
                 m["2fm", e] = rc(slot(e, 1, q, q), slot(e, 2, q, q), ss.at[7], rs.at[16 + e], dn2)
             sends = [m["1p"], m["1m"], m["1fp"], m["1fm"]]
             for k, b, off, size_k in ((4, 0, 0, size), (5, 0, 0, size), (6, 3, 0, q), (7, 1, q, q)):
-                r = slot(slice(None), b, off, size_k)
+                r = slot(slice(0, A1_SENDS if name == "a1" else 4), b, off, size_k)
                 sends.append(rc(r, r, ss.at[k], rs.at[4], up2))
+            m["start"] = []
+            for p in (0, 1):
+                o, n_ = p * q, q
+                m["start"].append([
+                    rc(slot(0, 0, o, n_), slot(3, 0, o, n_), ss.at[0], rs.at[0], up1),
+                    rc(slot(0, 0, o, n_), slot(1, 0, o, n_), ss.at[1], rs.at[1], dn1),
+                    rc(slot(0, 0, o, n_), slot(0, 3, o, n_), ss.at[4], rs.at[4], up2),
+                    rc(slot(0, 0, o, n_), slot(0, 1, o, n_), ss.at[5], rs.at[8], dn2)])
             m["sends"] = sends[:2] + sends[4:6] if name == "a1" else sends
             halves.append(m)
         return halves
@@ -125,8 +146,18 @@
     R = {name: ring(name) for name in RINGS}
 
     def t0(name):
-        for d in (1, 3) if name[0] == "a" else (2,):
-            xi(int(name[1]), d).wait_recv()
+        l = int(name[1])
+        if name == "a0":
+            for p in (0, 1):
+                for d in (1, 3):
+                    xi_part(d, p).wait_recv()
+                for k in range(4):
+                    for m in R[name]:
+                        m["start"][p][k].start()
+            return
+        if name[0] == "b":
+            for h in (0, 1):
+                xi2(l, h).wait_recv()
         for k in ("1p", "1m", ("2p", 0), ("2m", 0)):
             for m in R[name]:
                 m[k].start()
@@ -256,25 +287,33 @@
             xi(l, d).start()
 
     acc[...] = jnp.zeros_like(acc)
-    local[2].wait()
-    start_xi(0, (1, 3))
+    first[0].wait()
+    for p in (0, 1):
+        for d in (1, 3):
+            xi_part(d, p).start()
+    first[1].wait()
+    start_xi(1, (1, 3))
     pltpu.make_async_copy(im, im, im_sem).wait()
-    xa_send(1).start()
-    xa_send(3).start()
-    start_xi(0, (2,))
-    xa_send(2).start()
     xf(0).start()
     mine_x = pltpu.make_async_copy(im.at[:, xrow(x), :], X.at[xblk(x), xrow(c), :], l_sem.at[5])
     mine_x.start()
-    for cp in (local[0], local[1], local[3], mine_x):
+    local.append(mine_x)
+
+    t0("a0")
+    for h in (0, 1):
+        xi2(0, h).start()
+    for d in (1, 3, 2):
+        xa_send(d).start()
+    t1("a0")
+    for d in (1, 3):
+        xi(1, d).wait_recv()
+    for h in (0, 1):
+        xi2(1, h).start()
+    for cp in local:
         cp.wait()
-    start_xi(1, (2, 1, 3))
-    for k in range(len(FAR)):
+    for k in range(NF):
         for h in (0, 1):
             far(h, k).start()
-
-    t0("a0")
-    t1("a0")
     t3("a0", 0)
     t0("b0")
     t2("a0")
@@ -313,10 +352,6 @@
     t0("a1")
     t3("b1", 3)
     t3("b1", 1)
-    for h in (0, 1):
-        far(h, 0).wait_recv()
-        for k in ("2p", "2m"):
-            R["a1"][h][k, 2].start()
     for d in range(4):
         y1x(d, 1).wait_recv()
     comp_b(1, 1, lambda t: 0, lambda t: 1)
@@ -325,13 +360,14 @@
     t3("b1", 2)
     comp_b(1, 1, lambda t: 1, lambda t: 3)
     send_b([(1, 3), (3, 1)])
-    for k in range(1, len(FAR)):
+    for k in range(NF):
         for h in (0, 1):
             far(h, k).wait_recv()
     comp_a(1, 2, lambda t: 2 * t, lambda t: 0)
     send_a([(0, 0), (2, 0)])
     comp_a(1, 4, lambda t: t, lambda t: 2)
-    send_a([(0, 2), (1, 2), (2, 2), (3, 2)])
+    comp_a(1, 2, lambda t: 2, lambda t: 1 + 2 * t)
+    send_a([(0, 2), (1, 2), (2, 2), (3, 2), (2, 1), (2, 3)])
     for k in "pm":
         for m in R["a1"]:
             m["1" + k].wait_recv()
@@ -350,7 +386,7 @@
     own(1)
     for s in (0, 1):
         out_send(0, s, 0, half).start()
-    for e, ce in ((0, lambda t: 0), (2, lambda t: 2), (3, lambda t: 3), (1, lambda t: 1)):
+    for e, ce in ((0, lambda t: 0), (3, lambda t: 3), (1, lambda t: 1)):
         for k in "pm":
             for m in R["a1"]:
                 m["2" + k, e].wait_recv()
@@ -389,8 +425,10 @@
     for cp in cz + cy + cx:
         cp.wait_send()
     for l in range(2):
-        for d in (1, 2, 3):
+        for d in (1, 3):
             xi(l, d).wait_send()
+        for h in (0, 1):
+            xi2(l, h).wait_send()
     for h in (0, 1):
         for k in range(len(FAR)):
             far(h, k).wait_send()
@@ -440,17 +478,18 @@
             pltpu.VMEM((2 * NX, layers, T), jnp.float32),
             pltpu.SMEM(index.shape, jnp.int32),
             pltpu.VMEM(bias.shape, jnp.float32),
+            pltpu.VMEM((layers, kk, T), jnp.bfloat16),
             dma((8,)), dma((8,)),
-            dma((layers, 3)), dma((layers, 3)),
-            dma((2, 5)), dma((2, 5)),
+            dma((layers, 3)), dma((layers, 3)), dma((2, 2)), dma((layers, 2)), dma((layers, 2)),
+            dma((2, 7)), dma((2, 7)),
             dma((4, 2, 8)), dma((4, 2, 20)),
             dma((4,)), dma((4,)),
             dma((4, 2)), dma((4, 2)),
             dma((1,)), dma((1,)),
-            dma((6,)), dma,
+            dma((6,)), dma, dma((2,)),
             dma((20,)), dma((20,)),
         ],
-        compiler_params=pltpu.CompilerParams(collective_id=0, has_side_effects=True, vmem_limit_bytes=60 * 1024 * 1024),
+        compiler_params=pltpu.CompilerParams(collective_id=0, has_side_effects=True, vmem_limit_bytes=50 * 1024 * 1024),
         name="sparse_net",
     )(images, weights, index, bias)
 

time: 97.3 us -> 92.1 us (0.947)
  Pallas kernels: 92.9 us -> 87.9 us
    pallas_call x1, Pallas kernels: 92.9 us -> 87.9 us  [per_device(): pl.pallas_call(kernel, out_shape=(jax.ShapeDtypeStruct((n_img, cols), jnp...]
    unnamed x4 -> x6, local copies, waits for them, and re-layouts: 3.65 us -> 3.42 us
where the time goes in v3:
time: 92.1 us; the launch traced here: 92 us
  Pallas kernels  87.9 us (95%)
  local copies, waits for them, and re-layouts  3.42 us (4%)
    pallas_call x1, Pallas kernels, per_device(): pl.pallas_call(kernel, out_shape=(jax.ShapeDtypeStruct((n_img, cols), jnp...  87.9 us
    unnamed x6, local copies, waits for them, and re-layouts  3.42 us

profile of v3, /device:TPU:1, one launch (start us, length us, event | category | flops | bytes accessed | tf_op | source)
XLA Modules:
  0.0 92.0 jit_solution(4698427692769317447)
XLA Ops:
  0.6 0.0 copy-start
  0.6 0.9 copy-done
  1.5 0.0 copy-start.1
  1.5 0.7 copy-done.1
  2.2 87.9 %sparse_net.1 = (bf16[256,4096]{1,0:T(8,128)(2,1)S(1)}, f32[2]{0:T(128)S(1)}) custom-call(bf16[256,4096]{1,0:T(8,128)(2,1)} %img.1, bf16[2,32,512,128]{3,2,1,0:T(8,128)(2,1)} %w.1, s32[8,128]{1,0:T(8,128)S(1)} %bitcast.3, f32[2,16384]{1,0:T(2,128)S(1)} %copy-done), custom_call_target="tpu_custom_call" | custom-call | tf_op jit(solution)/shard_map/sparse_net/pallas_call | solution.py:462
  90.1 1.3 %copy.8 = bf16[256,4096]{1,0:T(8,128)(2,1)} copy(bf16[256,4096]{1,0:T(8,128)(2,1)S(1)} %get-tuple-element.4) | data formatting | bytes 4194304
  91.4 0.5 copy.9
Async XLA Ops:
  0.6 0.9 copy-start
  1.5 0.7 copy-start.1

commit v4 on v3

--- a/solution.py
+++ b/solution.py
@@ -15,7 +15,7 @@
 RINGS = {"a0": 0, "b0": 1, "b1": 2, "a1": 3}
 
 
-def kernel(img, w, bi_hbm, bias_hbm, out, stat, im, X, Y1, Wb, Wo, Ob, acc, accr, rz, ry, rx, bi, bias, Wx,
+def kernel(img, w, bi_hbm, bias_hbm, out, stat, im, X, Y1, Wb, Wo, Ob, acc, accr, rz, rx, bi, bias, Wx,
            x_ss, x_rs, xi_ss, xi_rs, xp_rs, x2_ss, x2_rs, far_ss, far_rs, w_ss, w_rs, y_ss, y_rs, o_ss, o_rs, a_ss, a_rs, l_sem, im_sem, wx_sem, z_ss, z_rs):
     x = lax.axis_index("nrn")
     i = lax.axis_index("img")
@@ -89,7 +89,7 @@
         r = pl.ds(h * (kk // 2), kk // 2)
         return rc(Wb.at[l, d - 1, 0, 0, r, :], Wb.at[l, 1, 0, 0, r, :], x2_ss.at[l, h], x2_rs.at[l, h], dev(dx=-d))
 
-    FAR = ((0, 2), (2, 2), (1, 2), (3, 2), (2, 0), (2, 1), (2, 3))
+    FAR = ((0, 2), (2, 2), (1, 2), (3, 2), (2, 0), (2, 3), (2, 1))
 
     NF = len(FAR)
 
@@ -97,7 +97,8 @@
         a, b = FAR[k]
         d = (1, 3)[h]
         ey, ez = (b, a) if h else (a, b)
-        return rc(Wo.at[1, place(ey, ez)], Wb.at[1, d - 1, ey, ez], far_ss.at[h, k], far_rs.at[h, k], dev(dx=-d))
+        r = pl.ds(0, kk) if k < 5 else pl.ds((k - 5) * (kk // 2), kk // 2)
+        return rc(Wo.at[1, place(ey, ez), r, :], Wb.at[1, d - 1, ey, ez, r, :], far_ss.at[h, k], far_rs.at[h, k], dev(dx=-d))
 
     def ring(name):
         n, l = RINGS[name], int(name[1])
@@ -127,6 +128,8 @@
                 m["2m", e] = rc(slot(e, 0, 0, size), slot(e, 1, 0, size), ss.at[5], rs.at[8 + e], dn2)
                 m["2fp", e] = rc(slot(e, 3, 0, q), slot(e, 2, 0, q), ss.at[6], rs.at[12 + e], up2)
                 m["2fm", e] = rc(slot(e, 1, q, q), slot(e, 2, q, q), ss.at[7], rs.at[16 + e], dn2)
+            m["hp"] = rc(slot(2, 0, q, q), slot(2, 3, q, q), ss.at[6], rs.at[6], up2)
+            m["hm"] = rc(slot(2, 0, 0, q), slot(2, 1, 0, q), ss.at[7], rs.at[10], dn2)
             sends = [m["1p"], m["1m"], m["1fp"], m["1fm"]]
             for k, b, off, size_k in ((4, 0, 0, size), (5, 0, 0, size), (6, 3, 0, q), (7, 1, q, q)):
                 r = slot(slice(0, A1_SENDS if name == "a1" else 4), b, off, size_k)
@@ -139,7 +142,7 @@
                     rc(slot(0, 0, o, n_), slot(1, 0, o, n_), ss.at[1], rs.at[1], dn1),
                     rc(slot(0, 0, o, n_), slot(0, 3, o, n_), ss.at[4], rs.at[4], up2),
                     rc(slot(0, 0, o, n_), slot(0, 1, o, n_), ss.at[5], rs.at[8], dn2)])
-            m["sends"] = sends[:2] + sends[4:6] if name == "a1" else sends
+            m["sends"] = sends[:2] + sends[4:6] + [m["hp"], m["hm"]] if name == "a1" else sends
             halves.append(m)
         return halves
 
@@ -363,11 +366,13 @@
     for k in range(NF):
         for h in (0, 1):
             far(h, k).wait_recv()
+    for k in ("hp", "hm"):
+        for m in R["a1"]:
+            m[k].start()
     comp_a(1, 2, lambda t: 2 * t, lambda t: 0)
     send_a([(0, 0), (2, 0)])
     comp_a(1, 4, lambda t: t, lambda t: 2)
-    comp_a(1, 2, lambda t: 2, lambda t: 1 + 2 * t)
-    send_a([(0, 2), (1, 2), (2, 2), (3, 2), (2, 1), (2, 3)])
+    send_a([(0, 2), (1, 2), (2, 2), (3, 2)])
     for k in "pm":
         for m in R["a1"]:
             m["1" + k].wait_recv()
@@ -383,6 +388,11 @@
     send_b([(0, 2), (2, 0), (0, 0), (1, 1), (2, 2), (3, 3), (1, 2), (2, 1), (3, 2), (2, 3)])
     comp_a(1, 2, lambda t: 1 + 2 * t, lambda t: 0)
     send_a([(1, 0), (3, 0)])
+    for k in ("hp", "hm"):
+        for m in R["a1"]:
+            m[k].wait_recv()
+    comp_a(1, 2, lambda t: 2, lambda t: 1 + 2 * t)
+    send_a([(2, 1), (2, 3)])
     own(1)
     for s in (0, 1):
         out_send(0, s, 0, half).start()
@@ -397,32 +407,31 @@
     ax.start()
     mine = acc[:, xrow(c), :]
     ax.wait_recv()
-    tot = jnp.sum(mine + accr[...], axis=2)
+    tot = jnp.sum(mine + accr[...], axis=2, keepdims=True)
     share = jnp.minimum(1.0, tot * (1.0 / (NX * cols * LIVE_LEVEL)))
-    part_sum = jnp.broadcast_to(jnp.sum(share, axis=1, keepdims=True), (2, T))
+    part_sum = jnp.broadcast_to(jnp.sum(share, axis=1, keepdims=True), (2, 1, T))
 
     def gather_sum(buf, n, me, val, targets, base):
-        buf[me] = val
+        for l in range(2):
+            buf[me, l:l + 1, :] = val[l]
         cps = [rc(buf.at[me], buf.at[me], z_ss.at[base + k], z_rs.at[base + k], t) for k, (t, _) in enumerate(targets)]
         for cp in cps:
             cp.start()
         for k, (_, who) in enumerate(targets):
             rc(buf.at[who], buf.at[who], z_ss.at[base + k], z_rs.at[base + k], dev(s=1)).wait_recv()
-        total = buf[0]
-        for k in range(1, n):
-            total = total + buf[k]
+        total = jnp.sum(buf[...], axis=0)[:, None, :]
         return total, cps
 
-    far_first = sorted(range(1, NZ), key=lambda d: -min(d, NZ - d))
-    v, cz = gather_sum(rz, NZ, z, part_sum, [(dev(dz=d), (z - d + NZ) % NZ) for d in far_first], 0)
-    v, cy = gather_sum(ry, NY, y, v, [(dev(dy=d), (y - d + NY) % NY) for d in (2, 1, 3)], NZ)
+    plane = [(dev(dy=a, dz=b), ((y - a + NY) % NY) * NZ + (z - b + NZ) % NZ)
+             for b in (4, 3, 5, 2, 6, 1, 7, 0) for a in (2, 1, 3, 0) if a or b]
+    v, cz = gather_sum(rz, NY * NZ, y * NZ + z, part_sum, plane, 0)
     me_x = [(dev(dx=d, s=s), ((x - d + NX) % NX) * 2 + (c + s) % 2) for d in (2, 1, 3, 0) for s in (0, 1) if d or s]
-    v, cx = gather_sum(rx, 2 * NX, x * 2 + c, v, me_x, NZ + NY)
+    v, cx = gather_sum(rx, 2 * NX, x * 2 + c, v, me_x, NY * NZ)
     v = v * (1.0 / (NX * rows * 2 * NZ * NY))
     for l in range(2):
-        stat[l] = jnp.sum(v[l:l + 1, 0:1])
-
-    for cp in cz + cy + cx:
+        stat[l] = jnp.sum(v[l, 0:1, 0:1])
+
+    for cp in cz + cx:
         cp.wait_send()
     for l in range(2):
         for d in (1, 3):
@@ -473,8 +482,7 @@
             pltpu.VMEM((NX, 2 * rows, half * T), jnp.bfloat16),
             pltpu.VMEM((layers, 2 * rows, T), jnp.float32),
             pltpu.VMEM((layers, rows, T), jnp.float32),
-            pltpu.VMEM((NZ, layers, T), jnp.float32),
-            pltpu.VMEM((NY, layers, T), jnp.float32),
+            pltpu.VMEM((NY * NZ, layers, T), jnp.float32),
             pltpu.VMEM((2 * NX, layers, T), jnp.float32),
             pltpu.SMEM(index.shape, jnp.int32),
             pltpu.VMEM(bias.shape, jnp.float32),
@@ -487,7 +495,7 @@
             dma((4, 2)), dma((4, 2)),
             dma((1,)), dma((1,)),
             dma((6,)), dma, dma((2,)),
-            dma((20,)), dma((20,)),
+            dma((40,)), dma((40,)),
         ],
         compiler_params=pltpu.CompilerParams(collective_id=0, has_side_effects=True, vmem_limit_bytes=50 * 1024 * 1024),
         name="sparse_net",

time: 92.1 us -> 91.8 us (level)
  no operation moved by 1% of the time
where the time goes in v4:
time: 91.8 us; the launch traced here: 91.7 us
  Pallas kernels  87.6 us (95%)
  local copies, waits for them, and re-layouts  3.42 us (4%)
    pallas_call x1, Pallas kernels, per_device(): pl.pallas_call(kernel, out_shape=(jax.ShapeDtypeStruct((n_img, cols), jnp...  87.6 us
    unnamed x6, local copies, waits for them, and re-layouts  3.42 us

profile of v4, /device:TPU:1, one launch (start us, length us, event | category | flops | bytes accessed | tf_op | source)
XLA Modules:
  0.0 91.7 jit_solution(12799665722801296267)
XLA Ops:
  0.6 0.0 copy-start
  0.6 0.9 copy-done
  1.5 0.0 copy-start.1
  1.5 0.7 copy-done.1
  2.2 87.6 %sparse_net.1 = (bf16[256,4096]{1,0:T(8,128)(2,1)S(1)}, f32[2]{0:T(128)S(1)}) custom-call(bf16[256,4096]{1,0:T(8,128)(2,1)} %img.1, bf16[2,32,512,128]{3,2,1,0:T(8,128)(2,1)} %w.1, s32[8,128]{1,0:T(8,128)S(1)} %bitcast.3, f32[2,16384]{1,0:T(2,128)S(1)} %copy-done), custom_call_target="tpu_custom_call" | custom-call | tf_op jit(solution)/shard_map/sparse_net/pallas_call | solution.py:471
  89.8 1.3 %copy.8 = bf16[256,4096]{1,0:T(8,128)(2,1)} copy(bf16[256,4096]{1,0:T(8,128)(2,1)S(1)} %get-tuple-element.4) | data formatting | bytes 4194304
  91.2 0.5 copy.9
Async XLA Ops:
  0.6 0.9 copy-start
  1.5 0.7 copy-start.1
